TPU v7x, 8 devices: a whole 2x2x1 slice. The times are simulated.
8 devices in a mesh: dp: 1 (over z), tp: 8 (over x, y, core).
Axes of the slice: x: 2, y: 2, z: 1, core: 2. Of those that a mesh axis runs over, the one named last changes fastest.
Arguments:
- x: bfloat16 [64, 5120], P('dp')
- k_cache: bfloat16 [64, 4096, 8, 128], P('dp', None, 'tp')
- v_cache: bfloat16 [64, 4096, 8, 128], P('dp', None, 'tp')
- gain_a: bfloat16 [5120], replicated
- wq: bfloat16 [5120, 4096], P(None, 'tp')
- wo: bfloat16 [4096, 5120], P('tp')
- gain_m: bfloat16 [5120], replicated
- w_gate: bfloat16 [5120, 32768], P(None, 'tp')
- w_up: bfloat16 [5120, 32768], P(None, 'tp')
- w_down: bfloat16 [32768, 5120], P('tp')
Outputs:
- output: bfloat16 [64, 5120], P('dp')
All inputs are finite; a program needn't handle non-finite values.
Results may differ from a plain program's by a relative error of at most 0.017.
Values are sent between devices in bfloat16 or wider.
A program may use at most 2 GiB of HBM per device.

v0:
```python
import jax
import jax.numpy as jnp
from jax import lax
from jax.sharding import PartitionSpec as P

HEAD = 128
THETA = 10000


def normed(x, gain):
    wide = x.astype(jnp.float32)
    scale = lax.rsqrt(jnp.mean(wide * wide, -1, keepdims=True) + 1e-6)
    return (wide * scale * gain.astype(jnp.float32)).astype(jnp.bfloat16)


def turned(t, place, theta):
    half = t.shape[-1] // 2
    angle = place.astype(jnp.float32)[:, None] * theta ** (-jnp.arange(half, dtype=jnp.float32) / half)
    cos, sin = jnp.cos(angle)[:, None], jnp.sin(angle)[:, None]
    a, b = t[..., :half].astype(jnp.float32), t[..., half:].astype(jnp.float32)
    return jnp.concatenate([a * cos - b * sin, b * cos + a * sin], -1).astype(jnp.bfloat16)


def matmul(a, w):
    return jnp.dot(a, w, preferred_element_type=jnp.float32).astype(jnp.bfloat16)


def einsum(form, a, b):
    return jnp.einsum(form, a.astype(jnp.float32), b.astype(jnp.float32))


def seen_by(a, wq, k_cache, v_cache, head, theta):
    batch, cache, kv_heads = k_cache.shape[:3]
    place = jnp.full((batch,), cache - 1)
    q = turned(matmul(a, wq).reshape(batch, -1, head), place, theta).reshape(batch, kv_heads, -1, head)
    scores = einsum("bgsd,bugd->bgsu", q, k_cache) * head**-0.5
    weights = jax.nn.softmax(scores, -1).astype(jnp.bfloat16)
    return einsum("bgsu,bugd->bgsd", weights, v_cache).astype(jnp.bfloat16).reshape(batch, -1)


def hidden_of(b, w_gate, w_up):
    gate = jnp.dot(b, w_gate, preferred_element_type=jnp.float32)
    up = jnp.dot(b, w_up, preferred_element_type=jnp.float32)
    return (jax.nn.silu(gate) * up).astype(jnp.bfloat16)


def solution(mesh):
    def added(t, term):
        return (t.astype(jnp.float32) + lax.psum(term.astype(jnp.bfloat16), "tp").astype(jnp.float32)).astype(jnp.bfloat16)

    def step(x, k_cache, v_cache, gain_a, wq, wo, gain_m, w_gate, w_up, w_down):
        seen = seen_by(normed(x, gain_a), wq, k_cache, v_cache, HEAD, THETA)
        h = added(x, jnp.dot(seen, wo, preferred_element_type=jnp.float32))
        return added(h, jnp.dot(hidden_of(normed(h, gain_m), w_gate, w_up), w_down, preferred_element_type=jnp.float32))

    states, cache, columns, rows_of = P("dp", None), P("dp", None, "tp", None), P(None, "tp"), P("tp", None)
    return jax.shard_map(
        step,
        mesh=mesh,
        in_specs=(states, cache, cache, P(None), columns, rows_of, P(None), columns, columns, rows_of),
        out_specs=states,
        check_vma=False,
    )
```

profile of v0, /device:TPU:0, one launch (start us, length us, event | category | flops | bytes accessed | tf_op | source)
XLA Modules:
  0.0 220.7 jit_solution(14969855658544824365)
XLA Ops:
  6.5 0.0 all-reduce.3.cloned.1.call-start
  6.6 0.7 convert_element_type.66
  7.3 1.3 fusion.12
  8.6 3.8 %convolution_convert_fusion.2 = bf16[64,512]{1,0:T(8,128)(2,1)S(1)} fusion(bf16[5120,512]{1,0:T(8,128)(2,1)} %param.14, bf16[64,5120]{1,0:T(8,128)(2,1)} %param.10, f32[5120]{0:T(1024)S(1)} %convert_element_type.66, f32[64]{0:T(128)S(1)} %add_rsqrt_fusion.1), kind=kOutput, calls=%fused_computation.29 | convolution fusion | flops 336887808 | bytes 5984512 | tf_op jit(solution)/shard_map/dot_general | solution.py:25
  12.5 0.1 fusion.39
  12.6 0.1 pad_maximum_fusion
  12.7 27.7 %fusion.40 = (f32[64,4]{1,0:T(8,128)S(1)}, f32[64,4,4096]{2,1,0:T(4,128)}) fusion(bf16[64,4096,1,128]{3,1,2,0:T(8,128)(2,1)} %param.11, bf16[64,4,128]{2,0,1:T(8,128)(2,1)S(1)} %pad_maximum_fusion), kind=kOutput, calls=%fused_computation.51 | convolution fusion | flops 271585280 | bytes 71369728 | tf_op jit(solution)/shard_map/sub | solution.py:37
  40.5 23.9 %fusion.20 = bf16[64,4,128]{2,1,0:T(4,128)(2,1)S(1)} fusion(bf16[64,4096,1,128]{3,1,2,0:T(8,128)(2,1)} %param.12, f32[64,4,4096]{2,1,0:T(4,128)} %get-tuple-element.12, f32[64,4]{1,0:T(8,128)S(1)} %get-tuple-element.11), kind=kOutput, calls=%fused_computation.28 | convolution fusion | flops 270565376 | bytes 71369728 | tf_op jit(solution)/shard_map/bgsu,bugd->bgsd/dot_general | solution.py:29
  64.4 0.0 copy-start.1
  64.4 0.0 copy-start
  64.4 4.4 %convolution_convert_fusion.1 = bf16[64,5120]{1,0:T(8,128)(2,1)} fusion(bf16[512,5120]{1,0:T(8,128)(2,1)} %param.15, bf16[8,8,4,128]{3,2,1,0:T(4,128)(2,1)S(1)} %bitcast.22), kind=kOutput, calls=%fused_computation.7 | convolution fusion | flops 335872000 | bytes 5963776 | tf_op jit(solution)/shard_map/dot_general | solution.py:53
  68.8 0.0 all-reduce.3.cloned.1.call-update
  68.9 0.2 all-reduce.5.cloned.1.call-start
  69.1 0.0 copy-done.1
  69.1 46.4 %all-reduce.3.cloned.1.call-done = bf16[64,5120]{1,0:T(8,128)(2,1)} async-done(((bf16[64,5120]{1,0:T(8,128)(2,1)}), bf16[64,5120]{1,0:T(8,128)(2,1)}) %all-reduce.3.cloned.1.call-update) | async-done | bytes 655376 | tf_op jit(solution)/shard_map/psum | solution.py:49
  115.6 0.0 copy-done
  115.6 1.4 fusion.16
  117.0 16.8 %fusion.27 = f32[64,4096]{1,0:T(8,128)S(1)} fusion(bf16[5120,4096]{1,0:T(8,128)(2,1)} %param.17, bf16[64,5120]{1,0:T(8,128)(2,1)S(1)} %get-tuple-element.6, f32[5120]{0:T(1024)S(1)} %convert_element_type.77, f32[64]{0:T(128)S(1)} %add_rsqrt_fusion), kind=kOutput, calls=%fused_computation.32 | convolution fusion | flops 2685665280 | bytes 43667712 | tf_op jit(solution)/shard_map/dot_general | solution.py:42
  133.8 17.1 %fusion.10 = bf16[64,4096]{1,0:T(8,128)(2,1)S(1)} fusion(bf16[5120,4096]{1,0:T(8,128)(2,1)} %param.18, f32[64,4096]{1,0:T(8,128)S(1)} %fusion.27, bf16[64,5120]{1,0:T(8,128)(2,1)S(1)} %get-tuple-element.6, f32[5120]{0:T(1024)S(1)} %convert_element_type.77, f32[64]{0:T(128)S(1)} %add_rsqrt_fusion), kind=kOutput, calls=%fused_computation.11 | convolution fusion | flops 2687238144 | bytes 44192000 | tf_op jit(solution)/shard_map/dot_general | solution.py:43
  150.9 17.6 %convolution_convert_fusion = bf16[64,5120]{1,0:T(8,128)(2,1)} fusion(bf16[64,4096]{1,0:T(8,128)(2,1)S(1)} %fusion.10, bf16[4096,5120]{1,0:T(8,128)(2,1)} %param.19), kind=kOutput, calls=%fused_computation.6 | convolution fusion | flops 2684682240 | bytes 43122688 | tf_op jit(solution)/shard_map/dot_general | solution.py:54
  168.5 0.0 all-reduce.5.cloned.1.call-update
  168.6 43.2 %all-reduce.5.cloned.1.call-done = bf16[64,5120]{1,0:T(8,128)(2,1)} async-done(((bf16[64,5120]{1,0:T(8,128)(2,1)}), bf16[64,5120]{1,0:T(8,128)(2,1)}) %all-reduce.5.cloned.1.call-update) | async-done | bytes 655376 | tf_op jit(solution)/shard_map/psum | solution.py:49
  211.8 2.1 fusion.19
  (6 shorter events, 0.1 us)
Async XLA Ops:
  6.5 109.0 %all-reduce.3.cloned.1.call-start = ((), (), s32[]{:S(2)}) async-start(), calls=%async_computation | async-start | bytes 1310720 | tf_op jit(solution)/shard_map/psum | solution.py:49
  64.4 4.7 %copy-start.1 = (bf16[5120]{0:T(1024)(128)(2,1)S(1)}, bf16[5120]{0:T(1024)(128)(2,1)}, u32[]{:S(2)}) copy-start(bf16[5120]{0:T(1024)(128)(2,1)} %param.16) | copy-start | bytes 30724
  64.4 51.2 %copy-start = (bf16[64,5120]{1,0:T(8,128)(2,1)S(1)}, bf16[64,5120]{1,0:T(8,128)(2,1)}, u32[]{:S(2)}) copy-start(bf16[64,5120]{1,0:T(8,128)(2,1)} %param.10) | copy-start | bytes 1966084
  68.9 142.9 %all-reduce.5.cloned.1.call-start = ((), (), s32[]{:S(2)}) async-start(), calls=%async_computation.1 | async-start | bytes 1310720 | tf_op jit(solution)/shard_map/psum | solution.py:49
Sparse Core Ops, SparseCore 0:
  69.0 46.5 all-reduce.2
  168.7 43.0 all-reduce.4
where the time goes:
time: 221 us
  matrix products  111 us (50%)
  waiting for transfers between devices  89.7 us (41%)
  between operations  13.5 us (6%)
  other arithmetic  5.72 us (3%)
    psum x2, waiting for transfers between devices, added(): lax.psum(term.astype(jnp.bfloat16), 'tp').astype(jnp.float32)  89.7 us
    sub x1, matrix products, seen_by(): weights = jax.nn.softmax(scores, -1).astype(jnp.bfloat16)  27.7 us
    dot_general x1, matrix products, einsum(): return jnp.einsum(form, a.astype(jnp.float32), b.astype(jnp.float32))  23.9 us
    dot_general x1, matrix products, step(): jnp.dot(hidden_of(normed(h, gain_m), w_gate, w_up), w_down, preferred_ele...  17.6 us
    dot_general x1, matrix products, hidden_of(): up = jnp.dot(b, w_up, preferred_element_type=jnp.float32)  17.1 us
    dot_general x1, matrix products, hidden_of(): gate = jnp.dot(b, w_gate, preferred_element_type=jnp.float32)  16.8 us
  transfers between devices with their start and end apart: 2, of which 2 were waited for; matrix products, arithmetic and copies ran while one was open for 0% of the time, Pallas kernels for 0%

commit v1 on v0

v1 whole, which is shorter than its diff:
```python
import functools

import jax
import jax.numpy as jnp
import numpy as np
from jax import lax
from jax.experimental import pallas as pl
from jax.experimental.pallas import tpu as pltpu
from jax.sharding import PartitionSpec as P

BATCH = 64
CACHE = 4096
D = 5120
HEAD = 128
GROUP = 4
FF = 4096
THETA = 10000
DEV = 8
MESH = pl.DeviceIdType.MESH

PAIRS = BATCH // 2
RING = 4
SLOTS = 7
WIDE = 256
GU_STEPS = FF // WIDE
DN_STEPS = D // (2 * WIDE)
SUBS = D // WIDE
CHUNK = 16
CHUNKS = BATCH // CHUNK
STEPS = PAIRS // 2
SPC = CHUNK // 4
OWN = D // DEV
KEYS = 256
LAG = 4
LOG2E = 1.4426950408889634
F32, BF16 = jnp.float32, jnp.bfloat16


def rotary():
    half = HEAD // 2
    angle = (CACHE - 1) * np.float64(THETA) ** (-np.arange(half) / half)
    cos, sin = np.cos(angle), np.sin(angle)
    return np.stack([np.concatenate([cos, cos]), np.concatenate([-sin, sin])]).astype(np.float32)


def norm_rows(src, gain_ref, dst):
    step = 512
    total = jnp.zeros((16, 128), F32)
    for c in range(D // step):
        t = src(c * step, step).astype(F32)
        t = t * t
        for j in range(step // 128):
            total = total + t[:, j * 128 : (j + 1) * 128]
    scale = lax.rsqrt(jnp.sum(total, axis=1, keepdims=True) * (1.0 / D) + 1e-6)
    for c in range(D // step):
        t = src(c * step, step).astype(F32)
        dst(c * step, step, (t * scale * gain_ref[:, c * step : (c + 1) * step].astype(F32)).astype(BF16))


def kernel(
    x_hbm, k_hbm, v_hbm, ga_ref, rot_ref, wq_hbm, wo_hbm, gm_ref, wg_hbm, wu_hbm, wd_hbm, y_hbm,
    kbuf, vbuf, wbuf, wobuf, xbuf, abuf, hbuf, hid, qs, os, prob,
    rs_send, rs_own, rs_recv, y_send, y_own, y_recv, ybuf,
    x_sem, k_sem, v_sem, w_sem, wo_sem, out_sem,
    rs_ssem, rs_rsem, ag_ssem, ag_rsem, ys_ssem, ys_rsem, yg_ssem, yg_rsem,
):
    me = lax.axis_index("tp")
    chip, core = me // 2, me % 2

    def k_copy(i):
        return pltpu.make_async_copy(k_hbm.at[pl.ds(2 * i, 2)], kbuf.at[i % RING], k_sem.at[i % RING])

    def v_copy(i):
        return pltpu.make_async_copy(v_hbm.at[pl.ds(2 * i, 2)], vbuf.at[i % RING], v_sem.at[i % RING])

    def gu_copy(j, half):
        cols = pl.ds(pl.multiple_of(j * WIDE, WIDE), WIDE)
        return pltpu.make_async_copy((wg_hbm, wu_hbm)[half].at[:, cols], wbuf.at[j % SLOTS, half], w_sem.at[j % SLOTS, half])

    def dn_copy(j, half):
        cols = pl.ds(pl.multiple_of((j - GU_STEPS) * 2 * WIDE + half * WIDE, WIDE), WIDE)
        return pltpu.make_async_copy(wd_hbm.at[:, cols], wbuf.at[j % SLOTS, half, pl.ds(0, FF)], w_sem.at[j % SLOTS, half])

    def gu_start(j):
        gu_copy(j, 0).start()
        gu_copy(j, 1).start()

    def dn_start(j):
        dn_copy(j, 0).start()
        dn_copy(j, 1).start()

    def wq_copy(half):
        return pltpu.make_async_copy(
            wq_hbm.at[:, pl.ds(half * WIDE, WIDE)], wbuf.at[SLOTS - 1, half], w_sem.at[SLOTS - 1, half]
        )

    x_copy = pltpu.make_async_copy(x_hbm, xbuf, x_sem)
    wo_copy = pltpu.make_async_copy(wo_hbm, wobuf, wo_sem)
    x_copy.start()
    wq_copy(0).start()
    wq_copy(1).start()
    for i in range(RING):
        k_copy(i).start()
        v_copy(i).start()
    wo_copy.start()
    gu_start(0)

    barrier = pltpu.get_barrier_semaphore()
    for o in range(1, DEV):
        pl.semaphore_signal(barrier, inc=1, device_id={"tp": lax.rem(me + o, DEV)}, device_id_type=MESH)

    x_copy.wait()

    @pl.loop(0, BATCH // 16)
    def _(r):
        rows = pl.ds(pl.multiple_of(r * 16, 16), 16)

        def dst(c, n, v):
            abuf[rows, c : c + n] = v

        norm_rows(lambda c, n: xbuf[rows, c : c + n], ga_ref, dst)

    cos, sin = rot_ref[0:1, :], rot_ref[1:2, :]
    for half in range(2):
        wq_copy(half).wait()
        q = jnp.dot(abuf[...], wbuf[SLOTS - 1, half], preferred_element_type=F32).astype(BF16).astype(F32)
        for g in range(2):
            t = q[:, g * HEAD : (g + 1) * HEAD]
            t = t * cos + pltpu.roll(t, HEAD // 2, 1) * sin
            qs[pl.ds(2 * half + g, BATCH, stride=GROUP), :] = t.astype(BF16).astype(F32)

    pl.semaphore_wait(barrier, DEV - 1)

    upper = lax.broadcasted_iota(jnp.int32, (8, HEAD), 0) < GROUP

    def scores(i):
        slot = i % RING
        q = qs[pl.ds(pl.multiple_of(i * 8, 8), 8), :]
        q = jnp.concatenate([jnp.where(upper, q, 0.0), jnp.where(upper, 0.0, q)], axis=1).astype(BF16)
        parts = []
        for u in range(CACHE // KEYS):
            keys = slice(u * KEYS, (u + 1) * KEYS)
            k = jnp.concatenate([kbuf[slot, 0, keys, :], kbuf[slot, 1, keys, :]], axis=1)
            parts.append(
                lax.dot_general(q, k, (((1,), (1,)), ((), ())), preferred_element_type=F32) * (HEAD**-0.5 * LOG2E)
            )
        top = functools.reduce(jnp.maximum, parts)
        top = jnp.max(top, axis=1, keepdims=True)
        parts = [jnp.exp2(t - top) for t in parts]
        total = functools.reduce(jnp.add, parts)
        inverse = 1.0 / jnp.sum(total, axis=1, keepdims=True)
        for u, t in enumerate(parts):
            prob[i % 4, :, u * KEYS : (u + 1) * KEYS] = (t * inverse).astype(BF16)

    def mix(i):
        slot = i % RING
        out = jnp.zeros((8, 2 * HEAD), F32)
        for u in range(CACHE // KEYS):
            keys = slice(u * KEYS, (u + 1) * KEYS)
            v = jnp.concatenate([vbuf[slot, 0, keys, :], vbuf[slot, 1, keys, :]], axis=1)
            out = out + jnp.dot(prob[i % 4, :, keys], v, preferred_element_type=F32)
        os[pl.ds(pl.multiple_of(i * 8, 8), 8), :] = jnp.where(upper, out[:, :HEAD], out[:, HEAD:])

    def own_cols(d):
        return pl.ds(pl.multiple_of(d * OWN, 128), OWN)

    def rs_copy(c, o):
        return pltpu.make_async_remote_copy(
            src_ref=rs_send.at[c, o - 1], dst_ref=rs_recv.at[c, o - 1], send_sem=rs_ssem.at[c], recv_sem=rs_rsem.at[c],
            device_id={"tp": lax.rem(me + o, DEV)}, device_id_type=MESH,
        )

    def ag_copy(c, o):
        return pltpu.make_async_remote_copy(
            src_ref=hbuf.at[c, :, own_cols(me)], dst_ref=hbuf.at[c, :, own_cols(me)], send_sem=ag_ssem.at[c],
            recv_sem=ag_rsem.at[c], device_id={"tp": lax.rem(me + o, DEV)}, device_id_type=MESH,
        )

    def all_of(ref, sem):
        return pltpu.make_async_copy(ref, ref, sem)

    def h_terms(c):
        seen = jnp.concatenate(
            [os[pl.ds(c * CHUNK * GROUP + g, CHUNK, stride=GROUP), :] for g in range(GROUP)], axis=1
        ).astype(BF16)
        for o in list(range(1, DEV)) + [0]:
            t = jnp.dot(seen, wobuf[:, own_cols(lax.rem(me + o, DEV))], preferred_element_type=F32)
            if o:
                rs_send[c, o - 1] = t.astype(BF16)
                rs_copy(c, o).start()
            else:
                rs_own[c] = t

    def h_sum(c):
        all_of(rs_recv.at[c], rs_rsem.at[c]).wait()
        rows = pl.ds(pl.multiple_of(c * CHUNK, CHUNK), CHUNK)
        t = rs_own[c]
        for o in range(DEV - 1):
            t = t + rs_recv[c, o].astype(F32)
        hbuf[c, :, own_cols(me)] = (xbuf[rows, own_cols(me)].astype(F32) + t).astype(BF16)
        for o in range(1, DEV):
            ag_copy(c, o).start()

    def h_norm(c):
        all_of(rs_recv.at[c], ag_rsem.at[c]).wait()
        rows = pl.ds(pl.multiple_of(c * CHUNK, CHUNK), CHUNK)

        def dst(at, n, v):
            abuf[rows, at : at + n] = v

        norm_rows(lambda at, n: hbuf[c, :, at : at + n], gm_ref, dst)

    for p in range(2):
        k_copy(p).wait()
    for p in range(2):
        scores(p)
    for p in range(2):
        k_copy(RING + p).start()

    @pl.loop(1, STEPS)
    def _(i):
        for p in range(2):
            k_copy(2 * i + p).wait()
            v_copy(2 * i - 2 + p).wait()
        for p in range(2):
            scores(2 * i + p)
        for p in range(2):
            mix(2 * i - 2 + p)

        @pl.when(2 * i + RING < PAIRS)
        def _():
            for p in range(2):
                k_copy(2 * i + RING + p).start()

        @pl.when(2 * i - 2 + RING < PAIRS)
        def _():
            for p in range(2):
                v_copy(2 * i - 2 + RING + p).start()

        @pl.when(i >= STEPS - 2)
        def _():
            gu_start(i - STEPS + 3)

        @pl.when(i == SPC)
        def _():
            wo_copy.wait()

        @pl.when((i % SPC == 0) & (i >= SPC))
        def _():
            h_terms(i // SPC - 1)

        @pl.when((i % SPC == 1) & (i >= SPC))
        def _():
            h_sum(i // SPC - 1)

        @pl.when((i % SPC == 2) & (i >= SPC))
        def _():
            h_norm(i // SPC - 1)

    for p in range(2):
        v_copy(PAIRS - 2 + p).wait()
    for p in range(2):
        mix(PAIRS - 2 + p)
    for j in range(3, SLOTS):
        gu_start(j)
    h_terms(CHUNKS - 1)
    h_sum(CHUNKS - 1)
    h_norm(CHUNKS - 1)

    @pl.loop(0, GU_STEPS)
    def _(j):
        slot = j % SLOTS
        gu_copy(j, 0).wait()
        gu_copy(j, 1).wait()
        b = abuf[...]
        gate = jnp.dot(b, wbuf[slot, 0], preferred_element_type=F32)
        up = jnp.dot(b, wbuf[slot, 1], preferred_element_type=F32)
        hid[:, pl.ds(pl.multiple_of(j * WIDE, WIDE), WIDE)] = (jax.nn.silu(gate) * up).astype(BF16)

        @pl.when(j + SLOTS < GU_STEPS)
        def _():
            gu_start(j + SLOTS)

        @pl.when(j + SLOTS >= GU_STEPS)
        def _():
            dn_start(j + SLOTS)

    def y_place(m, d):
        return (
            pl.ds(pl.multiple_of((d // 2) * 16, 16), 16),
            pl.ds(pl.multiple_of(m * WIDE + (d % 2) * 128, 128), 128),
        )

    def ys_copy(m, o):
        d = lax.rem(me + o, DEV)
        return pltpu.make_async_remote_copy(
            src_ref=y_send.at[m, d], dst_ref=y_recv.at[m, o - 1], send_sem=ys_ssem, recv_sem=ys_rsem.at[m],
            device_id={"tp": d}, device_id_type=MESH,
        )

    def yg_copy(m, o):
        rows, cols = y_place(m, me)
        return pltpu.make_async_remote_copy(
            src_ref=ybuf.at[rows, cols], dst_ref=ybuf.at[rows, cols], send_sem=yg_ssem, recv_sem=yg_rsem.at[m],
            device_id={"tp": lax.rem(me + o, DEV)}, device_id_type=MESH,
        )

    def y_sum(m):
        all_of(y_recv.at[m], ys_rsem.at[m]).wait()
        rows, cols = y_place(m, me)
        t = y_own[m % (LAG + 1), me]
        for o in range(DEV - 1):
            t = t + y_recv[m, o].astype(F32)
        ybuf[rows, cols] = (hbuf[chip, :, cols].astype(F32) + t).astype(BF16)
        for o in range(1, DEV):
            yg_copy(m, o).start()

    @pl.loop(0, SUBS)
    def _(m):
        j, half = GU_STEPS + m // 2, m % 2
        slot = j % SLOTS
        pltpu.make_async_copy(wd_hbm.at[:, pl.ds(0, WIDE)], wbuf.at[slot, half, pl.ds(0, FF)], w_sem.at[slot, half]).wait()
        t = jnp.dot(hid[...], wbuf[slot, half, :FF], preferred_element_type=F32)
        for d in range(DEV):
            part = t[(d // 2) * 16 : (d // 2) * 16 + 16, (d % 2) * 128 : (d % 2) * 128 + 128]
            y_own[m % (LAG + 1), d] = part
            y_send[m, d] = part.astype(BF16)
        for o in range(1, DEV):
            ys_copy(m, o).start()

        @pl.when((half == 1) & (j + SLOTS < GU_STEPS + DN_STEPS))
        def _():
            dn_start(j + SLOTS)

        @pl.when(m >= LAG)
        def _():
            y_sum(m - LAG)

    @pl.loop(SUBS - LAG, SUBS)
    def _(m):
        y_sum(m)

    @pl.loop(0, SUBS)
    def _(m):
        all_of(y_recv.at[m], yg_rsem.at[m]).wait()

    out = pltpu.make_async_copy(ybuf, y_hbm, out_sem)
    out.start()

    for c in range(CHUNKS):
        all_of(rs_recv.at[c], rs_ssem.at[c]).wait()
        all_of(rs_recv.at[c], ag_ssem.at[c]).wait()
    all_of(y_recv, ys_ssem).wait()
    all_of(y_recv, yg_ssem).wait()
    out.wait()


def solution(mesh):
    def step(x, k_cache, v_cache, gain_a, wq, wo, gain_m, w_gate, w_up, w_down):
        hbm = pl.BlockSpec(memory_space=pltpu.HBM)
        vmem = pl.BlockSpec(memory_space=pltpu.VMEM)
        dma = pltpu.SemaphoreType.DMA
        return pl.pallas_call(
            kernel,
            out_shape=jax.ShapeDtypeStruct((BATCH, D), BF16),
            in_specs=[hbm, hbm, hbm, vmem, vmem, hbm, hbm, vmem, hbm, hbm, hbm],
            out_specs=hbm,
            scratch_shapes=[
                pltpu.VMEM((RING, 2, CACHE, HEAD), BF16),
                pltpu.VMEM((RING, 2, CACHE, HEAD), BF16),
                pltpu.VMEM((SLOTS, 2, D, WIDE), BF16),
                pltpu.VMEM((GROUP * HEAD, D), BF16),
                pltpu.VMEM((BATCH, D), BF16),
                pltpu.VMEM((BATCH, D), BF16),
                pltpu.VMEM((CHUNKS, CHUNK, D), BF16),
                pltpu.VMEM((BATCH, FF), BF16),
                pltpu.VMEM((BATCH * GROUP, HEAD), F32),
                pltpu.VMEM((BATCH * GROUP, HEAD), F32),
                pltpu.VMEM((4, 8, CACHE), BF16),
                pltpu.VMEM((CHUNKS, DEV - 1, CHUNK, OWN), BF16),
                pltpu.VMEM((CHUNKS, CHUNK, OWN), F32),
                pltpu.VMEM((CHUNKS, DEV - 1, CHUNK, OWN), BF16),
                pltpu.VMEM((SUBS, DEV, 16, 128), BF16),
                pltpu.VMEM((LAG + 1, DEV, 16, 128), F32),
                pltpu.VMEM((SUBS, DEV - 1, 16, 128), BF16),
                pltpu.VMEM((BATCH, D), BF16),
                dma, dma((RING,)), dma((RING,)), dma((SLOTS, 2)), dma, dma,
                dma((CHUNKS,)), dma((CHUNKS,)), dma((CHUNKS,)), dma((CHUNKS,)),
                dma, dma((SUBS,)), dma, dma((SUBS,)),
            ],
            compiler_params=pltpu.CompilerParams(
                collective_id=0, has_side_effects=True, vmem_limit_bytes=67043328
            ),
            name="layer",
        )(
            x, k_cache.reshape(BATCH, CACHE, HEAD), v_cache.reshape(BATCH, CACHE, HEAD), gain_a.reshape(1, D),
            jnp.asarray(rotary()), wq, wo, gain_m.reshape(1, D), w_gate, w_up, w_down,
        )

    states, cache, columns, rows_of = P("dp", None), P("dp", None, "tp", None), P(None, "tp"), P("tp", None)
    return jax.shard_map(
        step,
        mesh=mesh,
        in_specs=(states, cache, cache, P(None), columns, rows_of, P(None), columns, columns, rows_of),
        out_specs=states,
        check_vma=False,
    )
```

time: 221 us -> 113 us (0.51)
  matrix products: 111 us -> 0 us
  Pallas kernels: 0 us -> 108 us
  waiting for transfers between devices: 89.7 us -> 0 us
  between operations: 13.5 us -> 0.01 us
  other arithmetic: 5.72 us -> 0 us
  local copies, waits for them, and re-layouts: 0.14 us -> 4.6 us
    pallas_call x0 -> x1, Pallas kernels: none -> 108 us  [step(): pl.pallas_call(kernel, out_shape=jax.ShapeDtypeStruct((BATCH, D), BF16),...]
    psum x2 -> x0, waiting for transfers between devices: 89.7 us -> none  [added(): lax.psum(term.astype(jnp.bfloat16), 'tp').astype(jnp.float32)]
    dot_general x6 -> x0, matrix products: 83.7 us -> none  [the longest x1 23.9 us: einsum(): return jnp.einsum(form, a.astype(jnp.float32), b.astype(jnp.float32))]
    sub x1 -> x0, matrix products: 27.7 us -> none  [seen_by(): weights = jax.nn.softmax(scores, -1).astype(jnp.bfloat16)]
    convert_element_type x3 -> x0, other arithmetic: 2.79 us -> none  [the longest x1 2.07 us: added(): (t.astype(jnp.float32) + lax.psum(term.astype(jnp.bfloat16), 'tp').astype...]
    reduce_sum x2 -> x0, other arithmetic: 2.73 us -> none  [normed(): scale = lax.rsqrt(jnp.mean(wide * wide, -1, keepdims=True) + 1e-06)]
    reshape x1 -> x2, local copies, waits for them, and re-layouts: 0.02 us -> 2.63 us  [the longest x1 1.32 us: step(): gain_a.reshape(1, D)]
  transfers between devices with their start and end apart: 2 -> 0, of which waited for: 2 -> 0; matrix products, arithmetic and copies ran while one was open for 0% -> 0% of each run, Pallas kernels for 0% -> 0%
where the time goes in v1:
time: 113 us; the launch traced here: 112 us
  Pallas kernels  108 us (96%)
  local copies, waits for them, and re-layouts  4.6 us (4%)
    pallas_call x1, Pallas kernels, step(): pl.pallas_call(kernel, out_shape=jax.ShapeDtypeStruct((BATCH, D), BF16),...  108 us

profile of v1, /device:TPU:0, one launch (start us, length us, event | category | flops | bytes accessed | tf_op | source)
XLA Modules:
  0.0 112.4 jit_solution(221258175099493242)
XLA Ops:
  0.0 1.3 %reshape.14.ga_ref = bf16[1,5120]{1,0:T(2,128)(2,1)} reshape(bf16[5120]{0:T(1024)(128)(2,1)} %param.14) | data formatting | bytes 20480 | tf_op jit(solution)/shard_map/reshape | solution.py:396
  1.3 1.3 %reshape.15.gm_ref = bf16[1,5120]{1,0:T(2,128)(2,1)} reshape(bf16[5120]{0:T(1024)(128)(2,1)} %param.17) | data formatting | bytes 20480 | tf_op jit(solution)/shard_map/reshape | solution.py:397
  2.6 107.8 %layer.1 = bf16[64,5120]{1,0:T(8,128)(2,1)} custom-call(bf16[64,5120]{1,0:T(8,128)(2,1)} %x_hbm.1, bf16[64,4096,128]{2,1,0:T(8,128)(2,1)} %bitcast.k_hbm, bf16[64,4096,128]{2,1,0:T(8,128)(2,1)} %bitcast.1.v_hbm, bf16[1,5120]{1,0:T(2,128)(2,1)} %reshape.14.ga_ref, f32[2,128]{1,0:T(2,128)} %constant.2.clone.rot_ref, bf16[5120,512]{1,0:T(8,128)(2,1)} %wq_hbm.1, ...), custom_call_target="tpu_custom_call" | custom-call | tf_op jit(solution)/shard_map/layer/pallas_call | solution.py:363
  110.5 2.0 %copy.13 = bf16[64,5120]{1,0:T(8,128)(2,1)} copy(bf16[64,5120]{1,0:T(8,128)(2,1)} %layer.1) | data formatting | bytes 1310720
